TPU v7x, 32 devices: a whole 2x2x4 slice. The times are simulated.
32 devices in a mesh: dp: 8 (over z, y), tp: 4 (over x, core).
Axes of the slice: x: 2, y: 2, z: 4, core: 2. Of those that a mesh axis runs over, the one named last changes fastest.
Arguments:
- tokens: bfloat16 [768, 2880], P('dp', 'tp'), may hold values from -100 to 100
- attn_gain: float32 [2880], replicated, may hold values from 0.1 to 1.9
- w_query: bfloat16 [2880, 2048], P(None, 'tp'), may hold values from -0.109375 to 0.109375
- w_keyvalue: bfloat16 [2880, 8, 128], P(None, 'tp'), may hold values from -0.109375 to 0.109375
- attn_sinks: float32 [32], P('tp'), may hold values from 2 to 6
- w_out: bfloat16 [2048, 2880], P('tp'), may hold values from -0.125 to 0.125
- window_cache: bfloat16 [768, 8, 128, 128], P('dp', 'tp'), may hold values from -1000 to 1000
- positions: int32 [768], P('dp'), may hold values from 0 to 511
- moe_gain: float32 [2880], replicated, may hold values from 0.1 to 1.9
- router: bfloat16 [2880, 8], P('tp'), may hold values from -0.109375 to 0.109375
- gate_up: bfloat16 [8, 2880, 2, 2880], P('dp', None, None, 'tp'), may hold values from -0.109375 to 0.109375
- w_down: bfloat16 [8, 2880, 2880], P('dp', None, 'tp'), may hold values from -0.109375 to 0.109375
- expert_ids: int32 [768, 4], P('dp'), may hold values from 0 to 7, all different within a row; in each aligned block of 96 rows (0 to 95, 96 to 191, ...) at most 96 rows name the same one
Outputs:
- layer_out: float32 [768, 2880], P('dp', 'tp')
Inputs may be any that keep to these rules, and one draw needn't show every extreme that they name: `expert_ids`: each row names 4 different experts. Within the rows of one index of dp no expert is named by more than 96 rows, a bound that some of these blocks reach.
All inputs are finite; a program needn't handle non-finite values.
Results may differ from a plain program's by a relative error of at most 0.0066.
Values may be sent and summed in bfloat16 or wider, within the bound.
A program may use at most 128 MiB of HBM per device.

v0:
```python
import jax
import jax.numpy as jnp
from jax import lax
from jax.sharding import PartitionSpec as P

norm_eps = 1e-05
rope_base = 150000.0
glu_alpha = 1.702


def rope_tables(positions, head_size):
    half_size = head_size // 2
    exponent = jnp.arange(half_size, dtype=jnp.float32) * (2.0 / head_size)
    inverse = jnp.power(jnp.float32(rope_base), -exponent)
    angles = positions.astype(jnp.float32)[:, None] * inverse[None, :]
    return (jnp.cos(angles), jnp.sin(angles))


def rotate(values, cosine, sine_table):
    half_size = values.shape[-1] // 2
    first_half = values[..., :half_size]
    second_half = values[..., half_size:]
    return jnp.concatenate(
        [
            first_half * cosine - second_half * sine_table,
            second_half * cosine + first_half * sine_table,
        ],
        axis=-1,
    )


def on_device(
    tokens,
    attn_gain,
    w_query,
    w_keyvalue,
    attn_sinks,
    w_out,
    window_cache,
    positions,
    moe_gain,
    router,
    gate_up,
    w_down,
    expert_ids,
):
    tp_count = lax.axis_size("tp")
    dp_count = lax.axis_size("dp")
    seq_count, col_count = tokens.shape
    full_width = col_count * tp_count
    col_start = lax.axis_index("tp") * col_count
    head_size = w_keyvalue.shape[2] // 2
    kv_local = w_keyvalue.shape[1]
    q_local = w_query.shape[1] // head_size
    group_size = q_local // kv_local
    window = window_cache.shape[2]
    attn_slice = lax.dynamic_slice_in_dim(attn_gain, col_start, col_count)
    moe_slice = lax.dynamic_slice_in_dim(moe_gain, col_start, col_count)
    tok_wide = tokens.astype(jnp.float32)
    attn_sq = lax.psum(jnp.sum(tok_wide * tok_wide, axis=1), "tp")
    normed = (
        tok_wide * lax.rsqrt(attn_sq / full_width + norm_eps)[:, None] * attn_slice[None, :]
    ).astype(jnp.bfloat16)
    kv_flat = w_keyvalue.reshape(full_width, kv_local * 2 * head_size)
    piece_rows = lax.all_gather(normed, "tp", axis=1, tiled=True)
    queries = jnp.dot(piece_rows, w_query, preferred_element_type=jnp.float32)
    fresh_rows = jnp.dot(piece_rows, kv_flat, preferred_element_type=jnp.float32)
    cosine, sine_table = rope_tables(positions, head_size)
    rot_queries = rotate(
        queries.reshape(seq_count, q_local, head_size), cosine[:, None, :], sine_table[:, None, :]
    ).astype(jnp.bfloat16)
    fresh_rows = fresh_rows.reshape(seq_count, kv_local, 2 * head_size)
    new_key = rotate(fresh_rows[..., :head_size], cosine[:, None, :], sine_table[:, None, :])
    new_entry = jnp.concatenate([new_key, fresh_rows[..., head_size:]], axis=-1).astype(
        jnp.bfloat16
    )
    slot_ids = jnp.arange(window, dtype=jnp.int32)
    is_current = slot_ids[None, :] == (positions % window)[:, None]
    cache_now = jnp.where(is_current[:, None, :, None], new_entry[:, :, None, :], window_cache)
    is_valid = (positions[:, None] - slot_ids[None, :]) % window <= positions[:, None]
    grouped = rot_queries.reshape(seq_count, kv_local, group_size, head_size)
    scores = jnp.einsum(
        "skgh,skwh->skgw", grouped, cache_now[..., :head_size], preferred_element_type=jnp.float32
    ) * head_size ** (-0.5)
    scores = jnp.where(is_valid[:, None, None, :], scores, -jnp.inf)
    sink_col = attn_sinks.reshape(kv_local, group_size)[None, :, :, None]
    peak_score = jnp.maximum(jnp.max(scores, axis=-1, keepdims=True), sink_col)
    raised = jnp.exp(scores - peak_score)
    denominator = jnp.sum(raised, axis=-1, keepdims=True) + jnp.exp(sink_col - peak_score)
    prob_bf = (raised / denominator).astype(jnp.bfloat16)
    attended = jnp.einsum(
        "skgw,skwh->skgh", prob_bf, cache_now[..., head_size:], preferred_element_type=jnp.float32
    ).astype(jnp.bfloat16)
    partial_out = jnp.dot(
        attended.reshape(seq_count, q_local * head_size), w_out, preferred_element_type=jnp.float32
    )
    residual = tok_wide + lax.psum_scatter(
        partial_out.astype(jnp.bfloat16), "tp", scatter_dimension=1, tiled=True
    ).astype(jnp.float32)
    experts = router.shape[1]
    top_count = expert_ids.shape[1]
    local_experts = gate_up.shape[0]
    ff_local = gate_up.shape[3]
    capacity = min(seq_count, max(2, 8 * seq_count * top_count // (3 * experts)))
    moe_sq = jnp.sum(residual * residual, axis=1)
    router_wide = router.astype(jnp.float32)
    total_sq = lax.psum(moe_sq, "tp")
    moe_scale = lax.rsqrt(total_sq / full_width + norm_eps)[:, None]
    scaled = residual * moe_scale * moe_slice[None, :]
    logits = lax.psum(jnp.dot(scaled, router_wide, precision=lax.Precision.HIGHEST), "tp")
    hidden_rows = scaled.astype(jnp.bfloat16)
    expert_iota = jnp.arange(experts, dtype=jnp.int32)
    chosen = expert_ids[:, :, None] == expert_iota[None, None, :]
    picked = jnp.sum(jnp.where(chosen, logits[:, None, :], 0.0), axis=-1)
    raised_logits = jnp.exp(picked)
    route_weights = raised_logits / jnp.sum(raised_logits, axis=1, keepdims=True)
    assign = expert_ids.reshape(-1)
    onehot = (assign[:, None] == expert_iota[None, :]).astype(jnp.int32)
    earlier = jnp.cumsum(onehot, axis=0) - onehot
    slot_of = jnp.sum(earlier * onehot, axis=1)
    target = (assign * capacity + slot_of).reshape(seq_count, top_count)
    spot_ids = jnp.arange(experts * capacity, dtype=jnp.int32)
    slot_hits = target[:, :, None] == spot_ids[None, None, :]
    placer = jnp.transpose(jnp.any(slot_hits, axis=1)).astype(jnp.bfloat16)
    combiner = jnp.sum(jnp.where(slot_hits, route_weights[:, :, None], 0.0), axis=1)
    gate_up_flat = gate_up.reshape(local_experts, full_width, 2 * ff_local)
    placed = jnp.dot(placer, hidden_rows, preferred_element_type=jnp.float32).astype(jnp.bfloat16)
    mixed_in = jnp.einsum(
        "gecd,edf->gecf",
        lax.all_gather(
            lax.all_to_all(
                placed.reshape(dp_count, local_experts, capacity, hidden_rows.shape[1]),
                "dp",
                split_axis=0,
                concat_axis=0,
                tiled=True,
            ),
            "tp",
            axis=3,
            tiled=True,
        ),
        gate_up_flat,
        preferred_element_type=jnp.float32,
    )
    gate_part = mixed_in[..., :ff_local]
    up_part = mixed_in[..., ff_local:]
    act_rows = (gate_part * jax.nn.sigmoid(glu_alpha * gate_part) * (up_part + 1.0)).astype(
        jnp.bfloat16
    )
    answered = jnp.einsum(
        "gecf,efd->gecd",
        lax.all_gather(act_rows, "tp", axis=3, tiled=True),
        w_down,
        preferred_element_type=jnp.float32,
    ).astype(jnp.bfloat16)
    returned = lax.all_to_all(answered, "dp", split_axis=0, concat_axis=0, tiled=True)
    flat_back = returned.reshape(experts * capacity, col_count).astype(jnp.float32)
    moe_out = jnp.dot(combiner, flat_back, precision=lax.Precision.HIGHEST)
    return residual + moe_out


def solution(mesh):
    in_specs = (
        P("dp", "tp"),
        P(),
        P(None, "tp"),
        P(None, "tp", None),
        P("tp"),
        P("tp", None),
        P("dp", "tp", None, None),
        P("dp"),
        P(),
        P("tp", None),
        P("dp", None, None, "tp"),
        P("dp", None, "tp"),
        P("dp", None),
    )
    out_specs = P("dp", "tp")
    return jax.shard_map(
        on_device, mesh=mesh, in_specs=in_specs, out_specs=out_specs, check_vma=False
    )
```

profile of v0, /device:TPU:0, one launch (start us, length us, event | category | flops | bytes accessed | tf_op | source)
XLA Modules:
  0.0 306.0 jit_solution(1373459359515891442)
XLA Ops:
  6.6 1.2 fusion.37
  7.8 8.4 %psum.21 = f32[96]{0:T(128)S(1)} all-reduce(f32[96]{0:T(128)S(1)} %fusion.37), channel_id=1, replica_groups=mesh['dp'=8,'tp'=4] {'tp'}, use_global_device_ids=true, to_apply=%region_1.0 | all-reduce | flops 96 | bytes 768 | tf_op jit(solution)/shard_map/psum | solution.py:60
  16.1 0.8 dynamic_slice.6
  16.9 1.0 fusion.48
  17.9 6.7 %all-gather = bf16[4,720,96]{1,2,0:T(8,128)(2,1)S(1)} all-gather(bf16[1,720,96]{1,2,0:T(8,128)(2,1)S(1)} %fusion.48), channel_id=1, replica_groups=mesh['dp'=8,'tp'=4] {'tp'}, dimensions={0}, use_global_device_ids=true | all-gather | bytes 691200 | tf_op jit(solution)/shard_map/all_gather | solution.py:65
  24.6 0.5 copy.86
  25.1 1.3 reshape.248
  26.4 1.3 reshape.247
  27.6 0.5 fusion.63
  28.2 0.7 fusion.54
  28.9 4.9 %copy.111 = bf16[2880,2,128]{0,2,1:T(8,128)(2,1)} copy(bf16[2880,2,128]{2,1,0:T(2,128)(2,1)} %param.16) | data formatting | bytes 2949120 | tf_op jit(solution)/shard_map/dot_general | solution.py:67
  33.9 0.7 copy.92
  34.6 0.7 copy.93
  35.3 2.0 fusion.19
  37.4 0.9 subtract_convert_fusion.1
  38.4 0.7 copy.94
  39.1 1.3 iota_compare_fusion.1
  40.4 8.7 %copy.95 = bf16[96,2,128,128]{2,3,1,0:T(8,128)(2,1)} copy(bf16[96,2,128,128]{3,2,1,0:T(8,128)(2,1)} %param.19) | data formatting | bytes 12582912 | tf_op args[6]
  49.1 3.1 %fusion.65 = f32[96,512]{0,1:T(8,128)S(1)} fusion(bf16[2880,96]{0,1:T(8,128)(2,1)S(1)} %copy-done.3, bf16[2880,512]{1,0:T(8,128)(2,1)} %param.15), kind=kOutput, calls=%fused_computation.91 | convolution fusion | flops 283115520 | bytes 3698688 | tf_op jit(solution)/shard_map/dot_general | solution.py:66
  52.7 7.2 %broadcast_select_fusion = bf16[96,2,128,128]{2,3,1,0:T(8,128)(2,1)S(1)} fusion(bf16[96,2,128,128]{2,3,1,0:T(8,128)(2,1)} %copy.95, pred[96,128]{1,0:T(8,128)(4,1)} %iota_compare_fusion.1, bf16[96,2,128]{2,1,0:T(2,128)(2,1)} %copy.94), kind=kLoop, calls=%fused_computation | loop fusion | flops 3145728 | bytes 12644352 | tf_op jit(solution)/shard_map/jit(_where)/select_n | solution.py:79
  59.9 1.2 fusion.64
  61.2 0.6 fusion.36
  61.8 1.8 fusion.33
  63.8 1.9 convolution_convert_fusion
  65.7 2.2 copy.112
  68.3 0.8 dynamic_slice.7
  69.1 0.8 reduce-window.6
  70.5 0.2 fusion.32
  70.7 21.4 %reduce-scatter.4.cloned.1.call-done = bf16[720,96]{1,0:T(8,128)(2,1)} async-done(((bf16[2880,96]{1,0:T(8,128)(2,1)}), bf16[720,96]{1,0:T(8,128)(2,1)}) %reduce-scatter.4.cloned.1.call-update) | async-done | bytes 138256
  92.1 1.0 copy.113
  93.3 5.8 %psum.22 = f32[96]{0:T(128)S(1)} all-reduce(f32[96]{0:T(128)S(1)} %multiply_reduce_fusion), channel_id=1, replica_groups=mesh['dp'=8,'tp'=4] {'tp'}, use_global_device_ids=true, to_apply=%region_9.10 | all-reduce | flops 96 | bytes 768 | tf_op jit(solution)/shard_map/psum | solution.py:107
  99.1 0.6 convolution_convert_fusion.1
  99.7 0.6 copy.100
  100.3 34.2 %all_to_all.10 = bf16[8,1,96,720]{3,2,1,0:T(8,128)(2,1)S(1)} all-to-all(bf16[8,1,96,720]{3,2,1,0:T(8,128)(2,1)S(1)} %bitcast.88), channel_id=1, replica_groups=mesh['dp'=8,'tp'=4] {'dp'}, dimensions={0} | all-to-all | bytes 2211840 | tf_op jit(solution)/shard_map/all_to_all | solution.py:131
  134.5 1.9 copy.102
  136.7 41.8 %all-gather.4.cloned.1.call-done = bf16[8,1,96,2880]{2,0,1,3:T(8,128)(2,1)} async-done(((bf16[8,1,96,720]{2,0,1,3:T(8,128)(2,1)}), bf16[8,1,96,2880]{2,0,1,3:T(8,128)(2,1)}) %all-gather.4.cloned.1.call-update) | async-done | bytes 4423696 | tf_op jit(solution)/shard_map/all_gather | solution.py:130
  178.5 8.3 %copy.103 = bf16[8,1,96,2880]{3,2,0,1:T(8,128)(2,1)} copy(bf16[8,1,96,2880]{2,0,1,3:T(8,128)(2,1)} %all-gather.4.cloned.1.call-done) | data formatting | bytes 8847360 | tf_op jit(solution)/shard_map/all_gather | solution.py:130
  186.8 11.4 %fusion.5 = f32[8,1,96,1440]{3,2,0,1:T(8,128)S(1)} fusion(bf16[2880,1440,1]{0,1,2:T(8,128)(2,1)} %bitcast.104, bf16[8,1,96,2880]{3,2,0,1:T(8,128)(2,1)} %copy.103), kind=kOutput, calls=%fused_computation.6 | convolution fusion | flops 6370099200 | bytes 17141760 | tf_op jit(solution)/shard_map/gecd,edf->gecf/dot_general | solution.py:128
  198.2 0.8 fusion.13
  199.1 1.9 copy.104
  201.0 44.3 %all-gather.6.cloned.1.call-done = bf16[8,1,96,2880]{2,0,1,3:T(8,128)(2,1)} async-done(((bf16[8,1,96,720]{2,0,1,3:T(8,128)(2,1)}), bf16[8,1,96,2880]{2,0,1,3:T(8,128)(2,1)}) %all-gather.6.cloned.1.call-update) | async-done | bytes 4423696 | tf_op jit(solution)/shard_map/all_gather | solution.py:152
  245.3 8.3 %copy.105 = bf16[8,1,96,2880]{3,2,0,1:T(8,128)(2,1)} copy(bf16[8,1,96,2880]{2,0,1,3:T(8,128)(2,1)} %all-gather.6.cloned.1.call-done) | data formatting | bytes 8847360 | tf_op jit(solution)/shard_map/all_gather | solution.py:152
  253.6 8.6 %fusion.21 = bf16[8,1,96,720]{3,2,1,0:T(8,128)(2,1)} fusion(bf16[1,2880,720]{1,2,0:T(8,128)(2,1)} %param.24, bf16[8,1,96,2880]{3,2,0,1:T(8,128)(2,1)} %copy.105), kind=kOutput, calls=%fused_computation.19 | convolution fusion | flops 3185602560 | bytes 9676800 | tf_op jit(solution)/shard_map/gecf,efd->gecd/dot_general | solution.py:150
  262.2 5.5 %all-to-all-start.1 = ((bf16[8,1,96,720]{3,2,1,0:T(8,128)(2,1)}), bf16[8,1,96,720]{3,2,1,0:T(8,128)(2,1)}, u32[]{:S(2)}, u32[]{:S(2)}) async-start(bf16[8,1,96,720]{3,2,1,0:T(8,128)(2,1)} %fusion.21), calls=%async_computation.1 | async-start | bytes 2359296 | tf_op jit(solution)/shard_map/all_to_all | solution.py:156
  267.7 0.3 fusion.41
  268.0 6.2 %psum.23 = f32[96,8]{0,1:T(8,128)S(1)} all-reduce(f32[96,8]{0,1:T(8,128)S(1)} %fusion.41), channel_id=1, replica_groups=mesh['dp'=8,'tp'=4] {'tp'}, use_global_device_ids=true, to_apply=%region_10.11 | all-reduce | flops 768 | bytes 6144 | tf_op jit(solution)/shard_map/psum | solution.py:110
  274.5 22.3 %all-to-all-done.1 = bf16[8,1,96,720]{3,2,1,0:T(8,128)(2,1)} async-done(((bf16[8,1,96,720]{3,2,1,0:T(8,128)(2,1)}), bf16[8,1,96,720]{3,2,1,0:T(8,128)(2,1)}, u32[]{:S(2)}, u32[]{:S(2)}) %all-to-all-start.1) | async-done | bytes 1105952 | tf_op jit(solution)/shard_map/all_to_all | solution.py:156
  296.8 2.7 convolution_add_fusion
  (56 shorter events, 2.6 us)
Async XLA Ops:
  6.5 57.3 %copy-start = (bf16[512,2880]{0,1:T(8,128)(2,1)S(1)}, bf16[512,2880]{0,1:T(8,128)(2,1)}, u32[]{:S(2)}) copy-start(bf16[512,2880]{0,1:T(8,128)(2,1)} %param.18) | copy-start | bytes 8847364
  6.5 21.1 %copy-start.7 = (s32[96]{0:T(128)S(1)}, s32[96]{0:T(128)}, u32[]{:S(2)}) copy-start(s32[96]{0:T(128)} %param.20) | copy-start | bytes 1156
  6.5 85.6 %reduce-scatter.4.cloned.1.call-start = ((), (), s32[]{:S(2)}) async-start(), calls=%async_computation.5 | async-start | bytes 921600
  27.6 7.7 %copy-start.4 = (bf16[2880,96,1]{0,1,2:T(8,128)(2,1)S(1)}, bf16[2880,96,1]{0,1,2:T(8,128)(2,1)}, u32[]{:S(2)}) copy-start(bf16[2880,96,1]{0,1,2:T(8,128)(2,1)} %reshape.248) | copy-start | bytes 1658884
  40.4 8.7 %copy-start.3 = (bf16[2880,96]{0,1:T(8,128)(2,1)S(1)}, bf16[2880,96]{0,1:T(8,128)(2,1)}, u32[]{:S(2)}) copy-start(bf16[2880,96]{0,1:T(8,128)(2,1)} %reshape.247) | copy-start | bytes 1658884
  49.1 3.5 %copy-start.9 = (f32[8]{0:T(128)S(1)}, f32[8]{0:T(128)}, u32[]{:S(2)}) copy-start(f32[8]{0:T(128)} %param.17) | copy-start | bytes 100
  52.7 7.2 %copy-start.6 = (pred[96,128]{1,0:T(8,128)(4,1)S(1)}, pred[96,128]{1,0:T(8,128)(4,1)}, u32[]{:S(2)}) copy-start(pred[96,128]{1,0:T(8,128)(4,1)} %fusion.54) | copy-start | bytes 36868
  63.6 4.4 %copy-start.5 = (s32[96,4]{0,1:T(4,128)S(1)}, s32[96,4]{0,1:T(4,128)}, u32[]{:S(2)}) copy-start(s32[96,4]{0,1:T(4,128)} %param.25) | copy-start | bytes 4612
  63.8 29.4 %copy-start.2 = (bf16[96,720]{1,0:T(8,128)(2,1)S(1)}, bf16[96,720]{1,0:T(8,128)(2,1)}, u32[]{:S(2)}) copy-start(bf16[96,720]{1,0:T(8,128)(2,1)} %param.13) | copy-start | bytes 414724
  67.9 110.5 %all-gather.4.cloned.1.call-start = ((), (), s32[]{:S(2)}) async-start(), calls=%async_computation.3 | async-start | bytes 7372800 | tf_op jit(solution)/shard_map/all_gather | solution.py:130
  136.5 108.8 %all-gather.6.cloned.1.call-start = ((), (), s32[]{:S(2)}) async-start(), calls=%async_computation.4 | async-start | bytes 7372800 | tf_op jit(solution)/shard_map/all_gather | solution.py:152
  253.6 14.1 %copy-start.8 = (bf16[720,8]{0,1:T(8,128)(2,1)S(1)}, bf16[720,8]{0,1:T(8,128)(2,1)}, u32[]{:S(2)}) copy-start(bf16[720,8]{0,1:T(8,128)(2,1)} %param.22) | copy-start | bytes 34564
  253.6 45.9 %copy-start.1 = (bf16[512,2880]{0,1:T(8,128)(2,1)S(1)}, bf16[512,2880]{0,1:T(8,128)(2,1)}, u32[]{:S(2)}) copy-start(bf16[512,2880]{0,1:T(8,128)(2,1)} %param.18) | copy-start | bytes 8847364
  262.2 34.6 %all-to-all-start.1 = ((bf16[8,1,96,720]{3,2,1,0:T(8,128)(2,1)}), bf16[8,1,96,720]{3,2,1,0:T(8,128)(2,1)}, u32[]{:S(2)}, u32[]{:S(2)}) async-start(bf16[8,1,96,720]{3,2,1,0:T(8,128)(2,1)} %fusion.21), calls=%async_computation.1 | async-start | bytes 2359296 | tf_op jit(solution)/shard_map/all_to_all | solution.py:156
Sparse Core Ops, SparseCore 0:
  68.0 24.0 reduce-scatter.3
  136.6 41.8 all-gather.3
  201.1 44.1 all-gather.5
where the time goes:
time: 307 us; the launch traced here: 306 us
  waiting for transfers between devices  130 us (42%)
  blocking collectives  61.2 us (20%)
  local copies, waits for them, and re-layouts  46.1 us (15%)
  matrix products  33.5 us (11%)
  other arithmetic  16.2 us (5%)
  between operations  13.4 us (4%)
  starting transfers between devices  5.78 us (2%)
    all_gather x1, waiting for transfers between devices, on_device(): lax.all_gather(act_rows, 'tp', axis=3, tiled=True)  44.3 us
    all_gather x1, waiting for transfers between devices, on_device(): lax.all_gather(lax.all_to_all(placed.reshape(dp_count, local_experts, cap...  41.8 us
    all_to_all x1, blocking collectives, on_device(): lax.all_to_all(placed.reshape(dp_count, local_experts, capacity, hidden_r...  34.2 us
    all_to_all x1, waiting for transfers between devices, on_device(): lax.all_to_all(answered, 'dp', split_axis=0, concat_axis=0, tiled=True)  22.3 us
    unnamed x4, waiting for transfers between devices  21.5 us
    unnamed x28, local copies, waits for them, and re-layouts  14.7 us
    dot_general x1, matrix products, on_device(): jnp.einsum('gecd,edf->gecf', lax.all_gather(lax.all_to_all(placed.reshape...  11.4 us
    dot_general x1, matrix products, on_device(): jnp.einsum('gecf,efd->gecd', lax.all_gather(act_rows, 'tp', axis=3, tiled...  8.57 us
  transfers between devices with their start and end apart: 4, of which 4 were waited for; matrix products, arithmetic and copies ran while one was open for 1% of the time, Pallas kernels for 0%

commit v1 on v0

--- a/solution.py
+++ b/solution.py
@@ -6,6 +6,18 @@
 norm_eps = 1e-05
 rope_base = 150000.0
 glu_alpha = 1.702
+
+
+def ring_product(value, axis, dim, contribution):
+    size, index, span = (lax.axis_size(axis), lax.axis_index(axis), value.shape[dim])
+    ahead = [(i, (i + 1) % size) for i in range(size)]
+    block, subtotal = (value, None)
+    for step in range(size):
+        upcoming = lax.ppermute(block, axis, ahead) if step < size - 1 else None
+        take_in = contribution(block, (index - step) % size * span)
+        subtotal = take_in if subtotal is None else subtotal + take_in
+        block = upcoming
+    return subtotal
 
 
 def rope_tables(positions, head_size):
@@ -147,11 +159,16 @@
     act_rows = (gate_part * jax.nn.sigmoid(glu_alpha * gate_part) * (up_part + 1.0)).astype(
         jnp.bfloat16
     )
-    answered = jnp.einsum(
-        "gecf,efd->gecd",
-        lax.all_gather(act_rows, "tp", axis=3, tiled=True),
-        w_down,
-        preferred_element_type=jnp.float32,
+    answered = ring_product(
+        act_rows,
+        "tp",
+        3,
+        lambda own_block, offset: jnp.einsum(
+            "gecf,efd->gecd",
+            own_block,
+            lax.dynamic_slice_in_dim(w_down, offset, own_block.shape[3], axis=1),
+            preferred_element_type=jnp.float32,
+        ),
     ).astype(jnp.bfloat16)
     returned = lax.all_to_all(answered, "dp", split_axis=0, concat_axis=0, tiled=True)
     flat_back = returned.reshape(experts * capacity, col_count).astype(jnp.float32)

time: 307 us -> 294 us (0.958)
  local copies, waits for them, and re-layouts: 46.1 us -> 35.8 us
  waiting for transfers between devices: 130 us -> 123 us
  matrix products: 33.5 us -> 37 us
    all_gather x1 -> x0, waiting for transfers between devices: 44.3 us -> none  [on_device(): lax.all_gather(act_rows, 'tp', axis=3, tiled=True)]
    ppermute x0 -> x3, waiting for transfers between devices: none -> 39.1 us  [ring_product(): upcoming = lax.ppermute(block, axis, ahead) if step < size - 1 else None]
    all_gather x1 -> x0, local copies, waits for them, and re-layouts: 8.35 us -> none  [on_device(): lax.all_gather(act_rows, 'tp', axis=3, tiled=True)]
    dot_general x1 -> x4, matrix products: 8.57 us -> 12 us  [on_device(): jnp.einsum('gecf,efd->gecd', own_block, lax.dynamic_slice_in_dim(w_down,...]
    unnamed x4 -> x3, waiting for transfers between devices: 21.5 us -> 21.4 us
  transfers between devices with their start and end apart: 4 -> 6, of which waited for: 4 -> 6; matrix products, arithmetic and copies ran while one was open for 1% -> 4% of each run, Pallas kernels for 0% -> 0%
where the time goes in v1:
time: 294 us; the launch traced here: 293 us
  waiting for transfers between devices  123 us (42%)
  blocking collectives  61.1 us (21%)
  matrix products  37 us (13%)
  local copies, waits for them, and re-layouts  35.8 us (12%)
  other arithmetic  16.2 us (6%)
  between operations  13.7 us (5%)
  starting transfers between devices  6 us (2%)
    all_gather x1, waiting for transfers between devices, on_device(): lax.all_gather(lax.all_to_all(placed.reshape(dp_count, local_experts, cap...  42 us
    ppermute x3, waiting for transfers between devices, ring_product(): upcoming = lax.ppermute(block, axis, ahead) if step < size - 1 else None  39.1 us
    all_to_all x1, blocking collectives, on_device(): lax.all_to_all(placed.reshape(dp_count, local_experts, capacity, hidden_r...  34.2 us
    unnamed x3, waiting for transfers between devices  21.4 us
    all_to_all x1, waiting for transfers between devices, on_device(): lax.all_to_all(answered, 'dp', split_axis=0, concat_axis=0, tiled=True)  20.6 us
    unnamed x28, local copies, waits for them, and re-layouts  14.7 us
    dot_general x4, matrix products, on_device(): jnp.einsum('gecf,efd->gecd', own_block, lax.dynamic_slice_in_dim(w_down,...  12 us
    dot_general x1, matrix products, on_device(): jnp.einsum('gecd,edf->gecf', lax.all_gather(lax.all_to_all(placed.reshape...  11.4 us
  transfers between devices with their start and end apart: 6, of which 6 were waited for; matrix products, arithmetic and copies ran while one was open for 4% of the time, Pallas kernels for 0%

profile of v1, /device:TPU:0, one launch (start us, length us, event | category | flops | bytes accessed | tf_op | source)
XLA Modules:
  0.0 293.0 jit_solution(1018665786642896984)
XLA Ops:
  6.6 1.2 fusion.40
  7.8 8.4 %psum.21 = f32[96]{0:T(128)S(1)} all-reduce(f32[96]{0:T(128)S(1)} %fusion.40), channel_id=1, replica_groups=mesh['dp'=8,'tp'=4] {'tp'}, use_global_device_ids=true, to_apply=%region_1.0 | all-reduce | flops 96 | bytes 768 | tf_op jit(solution)/shard_map/psum | solution.py:72
  16.1 0.8 dynamic_slice.18
  16.9 1.0 fusion.51
  17.9 6.7 %all-gather = bf16[4,720,96]{1,2,0:T(8,128)(2,1)S(1)} all-gather(bf16[1,720,96]{1,2,0:T(8,128)(2,1)S(1)} %fusion.51), channel_id=1, replica_groups=mesh['dp'=8,'tp'=4] {'tp'}, dimensions={0}, use_global_device_ids=true | all-gather | bytes 691200 | tf_op jit(solution)/shard_map/all_gather | solution.py:77
  25.1 1.3 reshape.278
  26.4 1.3 reshape.277
  27.6 0.5 fusion.70
  28.2 0.7 fusion.57
  28.9 4.9 %copy.125 = bf16[2880,2,128]{0,2,1:T(8,128)(2,1)} copy(bf16[2880,2,128]{2,1,0:T(2,128)(2,1)} %param.16) | data formatting | bytes 2949120 | tf_op jit(solution)/shard_map/dot_general | solution.py:79
  33.9 0.7 copy.104
  34.6 0.7 copy.105
  35.3 2.0 fusion.11
  37.4 0.9 subtract_convert_fusion.1
  38.4 0.7 copy.106
  39.1 1.3 iota_compare_fusion.1
  40.4 8.7 %copy.107 = bf16[96,2,128,128]{2,3,1,0:T(8,128)(2,1)} copy(bf16[96,2,128,128]{3,2,1,0:T(8,128)(2,1)} %param.19) | data formatting | bytes 12582912 | tf_op args[6]
  49.1 3.1 %fusion.72 = f32[96,512]{0,1:T(8,128)S(1)} fusion(bf16[2880,96]{0,1:T(8,128)(2,1)S(1)} %copy-done.3, bf16[2880,512]{1,0:T(8,128)(2,1)} %param.15), kind=kOutput, calls=%fused_computation.107 | convolution fusion | flops 283115520 | bytes 3698688 | tf_op jit(solution)/shard_map/dot_general | solution.py:78
  52.7 7.2 %broadcast_select_fusion = bf16[96,2,128,128]{2,3,1,0:T(8,128)(2,1)S(1)} fusion(bf16[96,2,128,128]{2,3,1,0:T(8,128)(2,1)} %copy.107, pred[96,128]{1,0:T(8,128)(4,1)} %iota_compare_fusion.1, bf16[96,2,128]{2,1,0:T(2,128)(2,1)} %copy.106), kind=kLoop, calls=%fused_computation | loop fusion | flops 3145728 | bytes 12644352 | tf_op jit(solution)/shard_map/jit(_where)/select_n | solution.py:91
  59.9 1.2 fusion.71
  61.2 0.6 fusion.39
  61.8 1.8 fusion.28
  63.8 1.9 convolution_convert_fusion
  65.7 2.2 copy.126
  68.3 0.8 dynamic_slice.19
  69.1 0.8 reduce-window.6
  70.7 21.4 %reduce-scatter.4.cloned.1.call-done = bf16[720,96]{1,0:T(8,128)(2,1)} async-done(((bf16[2880,96]{1,0:T(8,128)(2,1)}), bf16[720,96]{1,0:T(8,128)(2,1)}) %reduce-scatter.4.cloned.1.call-update) | async-done | bytes 138256
  92.2 1.0 copy.127
  93.4 5.8 %psum.22 = f32[96]{0:T(128)S(1)} all-reduce(f32[96]{0:T(128)S(1)} %multiply_reduce_fusion), channel_id=1, replica_groups=mesh['dp'=8,'tp'=4] {'tp'}, use_global_device_ids=true, to_apply=%region_9.10 | all-reduce | flops 96 | bytes 768 | tf_op jit(solution)/shard_map/psum | solution.py:119
  99.1 0.6 convolution_convert_fusion.1
  99.7 0.6 copy.113
  100.3 34.2 %all_to_all.10 = bf16[8,1,96,720]{3,2,1,0:T(8,128)(2,1)S(1)} all-to-all(bf16[8,1,96,720]{3,2,1,0:T(8,128)(2,1)S(1)} %bitcast.103), channel_id=1, replica_groups=mesh['dp'=8,'tp'=4] {'dp'}, dimensions={0} | all-to-all | bytes 2211840 | tf_op jit(solution)/shard_map/all_to_all | solution.py:143
  134.6 1.9 copy.115
  136.5 42.0 %all-gather.3.cloned.1.call-done = bf16[8,1,96,2880]{2,0,1,3:T(8,128)(2,1)} async-done(((bf16[8,1,96,720]{2,0,1,3:T(8,128)(2,1)}), bf16[8,1,96,2880]{2,0,1,3:T(8,128)(2,1)}) %all-gather.3.cloned.1.call-update) | async-done | bytes 4423696 | tf_op jit(solution)/shard_map/all_gather | solution.py:142
  178.5 8.3 %copy.116 = bf16[8,1,96,2880]{3,2,0,1:T(8,128)(2,1)} copy(bf16[8,1,96,2880]{2,0,1,3:T(8,128)(2,1)} %all-gather.3.cloned.1.call-done) | data formatting | bytes 8847360 | tf_op jit(solution)/shard_map/all_gather | solution.py:142
  186.8 11.4 %fusion.2 = f32[8,1,96,1440]{3,2,0,1:T(8,128)S(1)} fusion(bf16[2880,1440,1]{0,1,2:T(8,128)(2,1)} %bitcast.119, bf16[8,1,96,2880]{3,2,0,1:T(8,128)(2,1)} %copy.116), kind=kOutput, calls=%fused_computation.3 | convolution fusion | flops 6370099200 | bytes 17141760 | tf_op jit(solution)/shard_map/gecd,edf->gecf/dot_general | solution.py:140
  198.2 0.8 fusion.10
  199.4 15.4 %collective-permute-done = bf16[8,1,96,720]{3,2,0,1:T(8,128)(2,1)S(1)} collective-permute-done((bf16[8,1,96,720]{3,2,0,1:T(8,128)(2,1)S(1)}, bf16[8,1,96,720]{3,2,0,1:T(8,128)(2,1)S(1)}, u32[]{:S(2)}, u32[]{:S(2)}) %collective-permute-start) | collective-permute-done | bytes 1105952 | tf_op jit(solution)/shard_map/ppermute | solution.py:16
  214.8 15.7 %collective-permute-done.1 = bf16[8,1,96,720]{3,2,0,1:T(8,128)(2,1)} collective-permute-done((bf16[8,1,96,720]{3,2,0,1:T(8,128)(2,1)S(1)}, bf16[8,1,96,720]{3,2,0,1:T(8,128)(2,1)}, u32[]{:S(2)}, u32[]{:S(2)}) %collective-permute-start.1) | collective-permute-done | bytes 1105952 | tf_op jit(solution)/shard_map/ppermute | solution.py:16
  230.5 2.5 fusion.25
  233.0 2.5 fusion.23
  235.5 2.9 fusion.21
  238.4 8.0 %collective-permute-done.2 = bf16[8,1,96,720]{3,2,0,1:T(8,128)(2,1)} collective-permute-done((bf16[8,1,96,720]{3,2,0,1:T(8,128)(2,1)}, bf16[8,1,96,720]{3,2,0,1:T(8,128)(2,1)}, u32[]{:S(2)}, u32[]{:S(2)}) %collective-permute-start.2) | collective-permute-done | bytes 1105952 | tf_op jit(solution)/shard_map/ppermute | solution.py:16
  246.4 4.1 %fusion.13 = bf16[8,1,96,720]{3,2,1,0:T(8,128)(2,1)} fusion(f32[720,8,96]{0,2,1:T(8,128)S(1)} %fusion.21, f32[720,8,96]{0,2,1:T(8,128)S(1)} %fusion.25, f32[720,8,96]{0,2,1:T(8,128)S(1)} %fusion.23, bf16[8,1,96,720]{3,2,0,1:T(8,128)(2,1)} %collective-permute-done.2, bf16[1,2880,720]{1,2,0:T(8,128)(2,1)} %param.24, s32[]{:T(128)S(6)} %select_n.81), kind=kOutput, calls=%fused_computation.16 | convolution fusion | flops 798474240 | bytes 10027012 | tf_op jit(solution)/shard_map/gecf,efd->gecd/dot_general | solution.py:166
  250.6 5.7 %all-to-all-start.1 = ((bf16[8,1,96,720]{3,2,1,0:T(8,128)(2,1)}), bf16[8,1,96,720]{3,2,1,0:T(8,128)(2,1)}, u32[]{:S(2)}, u32[]{:S(2)}) async-start(bf16[8,1,96,720]{3,2,1,0:T(8,128)(2,1)} %fusion.13), calls=%async_computation.1 | async-start | bytes 2359296 | tf_op jit(solution)/shard_map/all_to_all | solution.py:173
  256.5 6.1 %psum.23 = f32[96,8]{0,1:T(8,128)S(1)} all-reduce(f32[96,8]{0,1:T(8,128)S(1)} %fusion.44), channel_id=1, replica_groups=mesh['dp'=8,'tp'=4] {'tp'}, use_global_device_ids=true, to_apply=%region_10.11 | all-reduce | flops 768 | bytes 6144 | tf_op jit(solution)/shard_map/psum | solution.py:122
  262.9 20.6 %all-to-all-done.1 = bf16[8,1,96,720]{3,2,1,0:T(8,128)(2,1)} async-done(((bf16[8,1,96,720]{3,2,1,0:T(8,128)(2,1)}), bf16[8,1,96,720]{3,2,1,0:T(8,128)(2,1)}, u32[]{:S(2)}, u32[]{:S(2)}) %all-to-all-start.1) | async-done | bytes 1105952 | tf_op jit(solution)/shard_map/all_to_all | solution.py:173
  283.5 2.7 convolution_add_fusion
  (60 shorter events, 3.7 us)
Async XLA Ops:
  6.5 57.3 %copy-start = (bf16[512,2880]{0,1:T(8,128)(2,1)S(1)}, bf16[512,2880]{0,1:T(8,128)(2,1)}, u32[]{:S(2)}) copy-start(bf16[512,2880]{0,1:T(8,128)(2,1)} %param.18) | copy-start | bytes 8847364
  6.5 21.1 %copy-start.7 = (s32[96]{0:T(128)S(1)}, s32[96]{0:T(128)}, u32[]{:S(2)}) copy-start(s32[96]{0:T(128)} %param.20) | copy-start | bytes 1156
  6.5 85.6 %reduce-scatter.4.cloned.1.call-start = ((), (), s32[]{:S(2)}) async-start(), calls=%async_computation.4 | async-start | bytes 921600
  27.6 7.7 %copy-start.4 = (bf16[2880,96,1]{0,1,2:T(8,128)(2,1)S(1)}, bf16[2880,96,1]{0,1,2:T(8,128)(2,1)}, u32[]{:S(2)}) copy-start(bf16[2880,96,1]{0,1,2:T(8,128)(2,1)} %reshape.278) | copy-start | bytes 1658884
  40.4 8.7 %copy-start.3 = (bf16[2880,96]{0,1:T(8,128)(2,1)S(1)}, bf16[2880,96]{0,1:T(8,128)(2,1)}, u32[]{:S(2)}) copy-start(bf16[2880,96]{0,1:T(8,128)(2,1)} %reshape.277) | copy-start | bytes 1658884
  49.1 3.5 %copy-start.9 = (f32[8]{0:T(128)S(1)}, f32[8]{0:T(128)}, u32[]{:S(2)}) copy-start(f32[8]{0:T(128)} %param.17) | copy-start | bytes 100
  52.7 7.2 %copy-start.6 = (pred[96,128]{1,0:T(8,128)(4,1)S(1)}, pred[96,128]{1,0:T(8,128)(4,1)}, u32[]{:S(2)}) copy-start(pred[96,128]{1,0:T(8,128)(4,1)} %fusion.57) | copy-start | bytes 36868
  63.8 4.2 %copy-start.5 = (s32[96,4]{0,1:T(4,128)S(1)}, s32[96,4]{0,1:T(4,128)}, u32[]{:S(2)}) copy-start(s32[96,4]{0,1:T(4,128)} %param.25) | copy-start | bytes 4612
  63.8 29.4 %copy-start.2 = (bf16[96,720]{1,0:T(8,128)(2,1)S(1)}, bf16[96,720]{1,0:T(8,128)(2,1)}, u32[]{:S(2)}) copy-start(bf16[96,720]{1,0:T(8,128)(2,1)} %param.13) | copy-start | bytes 414724
  67.9 110.5 %all-gather.3.cloned.1.call-start = ((), (), s32[]{:S(2)}) async-start(), calls=%async_computation.3 | async-start | bytes 7372800 | tf_op jit(solution)/shard_map/all_gather | solution.py:142
  199.1 15.7 %collective-permute-start = (bf16[8,1,96,720]{3,2,0,1:T(8,128)(2,1)S(1)}, bf16[8,1,96,720]{3,2,0,1:T(8,128)(2,1)S(1)}, u32[]{:S(2)}, u32[]{:S(2)}) collective-permute-start(bf16[8,1,96,720]{3,2,0,1:T(8,128)(2,1)S(1)} %fusion.10), channel_id=1, source_target_pairs={{0,1},{1,2},{2,3},{3,0},{4,5},{5,6},{6,7},{7,4},{8,9},{9,10},{10,1... | collective-permute-start | bytes 3317768 | tf_op jit(solution)/shard_map/ppermute | solution.py:16
  214.8 15.7 %collective-permute-start.1 = (bf16[8,1,96,720]{3,2,0,1:T(8,128)(2,1)S(1)}, bf16[8,1,96,720]{3,2,0,1:T(8,128)(2,1)}, u32[]{:S(2)}, u32[]{:S(2)}) collective-permute-start(bf16[8,1,96,720]{3,2,0,1:T(8,128)(2,1)S(1)} %collective-permute-done), channel_id=1, source_target_pairs={{0,1},{1,2},{2,3},{3,0},{4,5},{5,6},{6,7},{7,4},{8,9},{9,10},{10,1... | collective-permute-start | bytes 3317768 | tf_op jit(solution)/shard_map/ppermute | solution.py:16
  230.5 15.9 %collective-permute-start.2 = (bf16[8,1,96,720]{3,2,0,1:T(8,128)(2,1)}, bf16[8,1,96,720]{3,2,0,1:T(8,128)(2,1)}, u32[]{:S(2)}, u32[]{:S(2)}) collective-permute-start(bf16[8,1,96,720]{3,2,0,1:T(8,128)(2,1)} %collective-permute-done.1), channel_id=1, source_target_pairs={{0,1},{1,2},{2,3},{3,0},{4,5},{5,6},{6,7},{7,4},{8,9},{9,10},{10,1... | collective-permute-start | bytes 3317768 | tf_op jit(solution)/shard_map/ppermute | solution.py:16
  246.4 39.7 %copy-start.1 = (bf16[512,2880]{0,1:T(8,128)(2,1)S(1)}, bf16[512,2880]{0,1:T(8,128)(2,1)}, u32[]{:S(2)}) copy-start(bf16[512,2880]{0,1:T(8,128)(2,1)} %param.18) | copy-start | bytes 8847364
  250.6 5.7 %copy-start.8 = (bf16[720,8]{0,1:T(8,128)(2,1)S(1)}, bf16[720,8]{0,1:T(8,128)(2,1)}, u32[]{:S(2)}) copy-start(bf16[720,8]{0,1:T(8,128)(2,1)} %param.22) | copy-start | bytes 34564
  250.6 32.9 %all-to-all-start.1 = ((bf16[8,1,96,720]{3,2,1,0:T(8,128)(2,1)}), bf16[8,1,96,720]{3,2,1,0:T(8,128)(2,1)}, u32[]{:S(2)}, u32[]{:S(2)}) async-start(bf16[8,1,96,720]{3,2,1,0:T(8,128)(2,1)} %fusion.13), calls=%async_computation.1 | async-start | bytes 2359296 | tf_op jit(solution)/shard_map/all_to_all | solution.py:173
Sparse Core Ops, SparseCore 0:
  68.0 24.0 reduce-scatter.3
  136.6 41.8 all-gather.2
